TPU v7x, 32 devices: a whole 2x2x4 slice. The times are simulated.
32 devices in a mesh: dp: 4 (over z), expert: 8 (over y, x, core).
Axes of the slice: x: 2, y: 2, z: 4, core: 2. Of those that a mesh axis runs over, the one named last changes fastest.
Arguments:
- tokens: bfloat16 [2, 12288, 768], P(None, ('dp', 'expert')), may hold values from -6 to 6
- cotangent: bfloat16 [2, 12288, 768], P(None, ('dp', 'expert')), may hold values from -6 to 6
- token_ids: int32 [2, 12288], P(None, ('dp', 'expert')), may hold values from 0 to 8007, as said below
- hash_table: int32 [8008], replicated, may hold values from 0 to 7, as said below
- segment_ids: int32 [2, 12288], P(None, ('dp', 'expert')), may hold values from 0 to 1, as said below
- query_weight: bfloat16 [768, 768], replicated, may hold values from -0.21875 to 0.21875
- key_weight: bfloat16 [768, 768], replicated, may hold values from -0.21875 to 0.21875
- value_weight: bfloat16 [768, 768], replicated, may hold values from -0.21875 to 0.21875
- output_weight: bfloat16 [768, 768], replicated, may hold values from -2.5 to 2.5
- gain_attn: float32 [768], replicated, may hold values from 0.5 to 1.5
- gain_ffn: float32 [768], replicated, may hold values from 0.5 to 1.5
- expert_in: bfloat16 [8, 768, 3072], P('expert'), may hold values from -0.21875 to 0.21875
- expert_out: bfloat16 [8, 3072, 768], P('expert'), may hold values from -0.109375 to 0.109375
Outputs:
- block_out: bfloat16 [2, 12288, 768], P(None, ('dp', 'expert'))
- grad_tokens: bfloat16 [2, 12288, 768], P(None, ('dp', 'expert'))
- grad_query: float32 [768, 768], replicated
- grad_key: float32 [768, 768], replicated
- grad_value: float32 [768, 768], replicated
- grad_output: float32 [768, 768], replicated
- grad_gain_attn: float32 [768], replicated
- grad_gain_ffn: float32 [768], replicated
- grad_expert_in: float32 [8, 768, 3072], P('expert')
- grad_expert_out: float32 [8, 3072, 768], P('expert')
Inputs may be any that keep to these rules, and one draw needn't show every extreme that they name: hash_table sends 8008 // 8 or more ids to every expert. `token_ids`: in every micro-batch the 384 tokens of one device name any expert, through hash_table, at most 96 times; in every micro-batch one expert is named exactly 96 times by the tokens of every device. `segment_ids`: in each micro-batch a device's block holds either one sequence (all 0) or a sequence of 256 tokens (0) followed by one of the rest (1).
All inputs are finite; a program needn't handle non-finite values.
Results may differ from a plain program's by a relative error of at most 0.012.
Values may be sent and summed in bfloat16 or wider, within the bound.
No kernel may reach another device: no remote copies, remote signals or barrier semaphores. Data moves between devices by JAX's collectives and lax.ppermute only.
A program may use at most 192 MiB of HBM per device.

v0:
```python
import jax
import jax.numpy as jnp
from jax import lax
from jax.sharding import PartitionSpec as P

HEADS = 12
HEAD_DIM = 64
epsilon = 1e-05


def normalize(values, gain):
    return values * lax.rsqrt(jnp.mean(values * values, axis=-1, keepdims=True) + epsilon) * gain


def smooth_slope(values):
    sigmoid_part = jax.nn.sigmoid(values)
    return sigmoid_part * (1.0 + values * (1.0 - sigmoid_part))


def split_heads(matrix, head_count):
    return matrix.reshape(matrix.shape[0], head_count, -1).transpose(1, 0, 2)


def merge_heads(tensor):
    return tensor.transpose(1, 0, 2).reshape(tensor.shape[1], -1)


def masked_scores(query_heads, key_heads, allowed, score_scale):
    scores = (
        jnp.einsum("hqd,hkd->hqk", query_heads, key_heads, preferred_element_type=jnp.float32)
        * score_scale
    )
    return jnp.where(allowed[None], scores, -1e30)


def per_device(
    tokens,
    cotangent,
    token_ids,
    hash_table,
    segment_ids,
    query_weight,
    key_weight,
    value_weight,
    output_weight,
    gain_attn,
    gain_ffn,
    expert_in,
    expert_out,
):
    batches = tokens.shape[0]
    length = tokens.shape[1]
    model_width = tokens.shape[2]
    owners = lax.axis_size("expert")
    capacity = 2 * length // owners
    head_count = HEADS
    score_scale = HEAD_DIM ** (-0.5)
    weight_in = expert_in[0]
    weight_out = expert_out[0]
    position = jnp.arange(length, dtype=jnp.int32)
    float_type = jnp.float32
    half_type = jnp.bfloat16
    dense_total = (
        jnp.zeros(query_weight.shape, float_type),
        jnp.zeros(key_weight.shape, float_type),
        jnp.zeros(value_weight.shape, float_type),
        jnp.zeros(output_weight.shape, float_type),
        jnp.zeros(gain_attn.shape, float_type),
        jnp.zeros(gain_ffn.shape, float_type),
    )
    grad_in_sum = jnp.zeros(weight_in.shape, float_type)
    grad_out_sum = jnp.zeros(weight_out.shape, float_type)
    outputs = []
    grads_in = []
    for batch in range(batches):
        inputs_f = tokens[batch].astype(float_type)
        segments = segment_ids[batch]
        allowed = (position[:, None] >= position[None, :]) & (
            segments[:, None] == segments[None, :]
        )
        normed_attn = normalize(inputs_f, gain_attn).astype(half_type)
        query_heads = split_heads(
            jnp.dot(normed_attn, query_weight, preferred_element_type=float_type).astype(half_type),
            head_count,
        )
        key_heads = split_heads(
            jnp.dot(normed_attn, key_weight, preferred_element_type=float_type).astype(half_type),
            head_count,
        )
        value_heads = split_heads(
            jnp.dot(normed_attn, value_weight, preferred_element_type=float_type).astype(half_type),
            head_count,
        )
        scores = masked_scores(query_heads, key_heads, allowed, score_scale)
        row_peak = jnp.max(scores, axis=-1, keepdims=True)
        log_total = row_peak + jnp.log(jnp.sum(jnp.exp(scores - row_peak), axis=-1, keepdims=True))
        probs_low = jnp.exp(scores - log_total).astype(half_type)
        attended = merge_heads(
            jnp.einsum("hqk,hkd->hqd", probs_low, value_heads, preferred_element_type=float_type)
        ).astype(half_type)
        hidden = inputs_f + jnp.dot(attended, output_weight, preferred_element_type=float_type)
        routed = normalize(hidden, gain_ffn).astype(half_type)
        experts = jnp.take(hash_table, token_ids[batch])
        onehot = (experts[:, None] == jnp.arange(owners, dtype=jnp.int32)[None, :]).astype(
            jnp.int32
        )
        rank = jnp.sum((jnp.cumsum(onehot, axis=0, dtype=jnp.int32) - onehot) * onehot, axis=1)
        slot_index = experts * capacity + rank
        packed = jnp.zeros((owners * capacity, model_width), half_type).at[slot_index].set(routed)
        packed = packed.reshape(owners, capacity, model_width)
        received = lax.all_to_all(
            packed, "expert", split_axis=0, concat_axis=0, tiled=True
        ).reshape(owners * capacity, model_width)
        pre_active = jnp.dot(received, weight_in, preferred_element_type=float_type)
        active = jax.nn.silu(pre_active).astype(half_type)
        produced = jnp.dot(active, weight_out, preferred_element_type=float_type).astype(half_type)
        returned = lax.all_to_all(
            produced.reshape(owners, capacity, model_width),
            "expert",
            split_axis=0,
            concat_axis=0,
            tiled=True,
        )
        returned = returned.reshape(owners * capacity, model_width)
        block_out = hidden + jnp.take(returned, slot_index, axis=0).astype(float_type)
        outputs.append(block_out.astype(half_type))
        grad_block = cotangent[batch].astype(float_type)
        grad_result = grad_block.astype(half_type)
        grad_packed = (
            jnp.zeros((owners * capacity, model_width), half_type).at[slot_index].set(grad_result)
        )
        grad_packed = grad_packed.reshape(owners, capacity, model_width)
        grad_recv = lax.all_to_all(grad_packed, "expert", split_axis=0, concat_axis=0, tiled=True)
        grad_recv = grad_recv.reshape(owners * capacity, model_width)
        slope = smooth_slope(pre_active)
        grad_out_sum = grad_out_sum + jnp.dot(
            active.T, grad_recv, preferred_element_type=float_type
        )
        grad_active = jnp.dot(grad_recv, weight_out.T, preferred_element_type=float_type)
        grad_pre = (grad_active * slope).astype(half_type)
        grad_in_sum = grad_in_sum + jnp.dot(received.T, grad_pre, preferred_element_type=float_type)
        grad_rows = jnp.dot(grad_pre, weight_in.T, preferred_element_type=float_type).astype(
            half_type
        )
        grad_back = lax.all_to_all(
            grad_rows.reshape(owners, capacity, model_width),
            "expert",
            split_axis=0,
            concat_axis=0,
            tiled=True,
        )
        grad_routed = jnp.take(
            grad_back.reshape(owners * capacity, model_width), slot_index, axis=0
        ).astype(float_type)
        ignored_ffn, pull_ffn = jax.vjp(normalize, hidden, gain_ffn)
        grad_from_ffn, grad_gain_two = pull_ffn(grad_routed)
        grad_hidden = grad_block + grad_from_ffn
        grad_attn = grad_hidden.astype(half_type)
        grad_output_term = jnp.dot(attended.T, grad_attn, preferred_element_type=float_type)
        grad_mixed = split_heads(
            jnp.dot(grad_attn, output_weight.T, preferred_element_type=float_type).astype(
                half_type
            ),
            head_count,
        )
        scores_again = masked_scores(query_heads, key_heads, allowed, score_scale)
        probs = jnp.exp(scores_again - log_total)
        probs_again = probs.astype(half_type)
        grad_values = jnp.einsum(
            "hqk,hqd->hkd", probs_again, grad_mixed, preferred_element_type=float_type
        ).astype(half_type)
        grad_probs = jnp.einsum(
            "hqd,hkd->hqk", grad_mixed, value_heads, preferred_element_type=float_type
        )
        shared = jnp.sum(probs * grad_probs, axis=-1, keepdims=True)
        grad_scores = (probs * (grad_probs - shared)).astype(half_type)
        grad_queries = (
            jnp.einsum("hqk,hkd->hqd", grad_scores, key_heads, preferred_element_type=float_type)
            * score_scale
        ).astype(half_type)
        grad_keys = (
            jnp.einsum("hqk,hqd->hkd", grad_scores, query_heads, preferred_element_type=float_type)
            * score_scale
        ).astype(half_type)
        grad_queries = merge_heads(grad_queries)
        grad_keys = merge_heads(grad_keys)
        grad_values = merge_heads(grad_values)
        grad_query_term = jnp.dot(normed_attn.T, grad_queries, preferred_element_type=float_type)
        grad_key_term = jnp.dot(normed_attn.T, grad_keys, preferred_element_type=float_type)
        grad_value_term = jnp.dot(normed_attn.T, grad_values, preferred_element_type=float_type)
        grad_normed = (
            jnp.dot(grad_queries, query_weight.T, preferred_element_type=float_type)
            + jnp.dot(grad_keys, key_weight.T, preferred_element_type=float_type)
            + jnp.dot(grad_values, value_weight.T, preferred_element_type=float_type)
        )
        ignored_attn, pull_attn = jax.vjp(normalize, inputs_f, gain_attn)
        grad_from_attn, grad_gain_one = pull_attn(grad_normed)
        grads_in.append((grad_hidden + grad_from_attn).astype(half_type))
        terms = (
            grad_query_term,
            grad_key_term,
            grad_value_term,
            grad_output_term,
            grad_gain_one,
            grad_gain_two,
        )
        dense_total = tuple((total + term for total, term in zip(dense_total, terms)))
    dense_total = lax.psum(
        (
            dense_total[0],
            dense_total[1],
            dense_total[2],
            dense_total[3],
            dense_total[4],
            dense_total[5],
        ),
        ("dp", "expert"),
    )
    expert_in_sum, expert_out_sum = (
        lax.psum(grad_in_sum.astype(jnp.bfloat16), "dp").astype(jnp.float32),
        lax.psum(grad_out_sum.astype(jnp.bfloat16), "dp").astype(jnp.float32),
    )
    return (
        jnp.stack(outputs),
        jnp.stack(grads_in),
        dense_total[0],
        dense_total[1],
        dense_total[2],
        dense_total[3],
        dense_total[4],
        dense_total[5],
        expert_in_sum[None],
        expert_out_sum[None],
    )


def solution(mesh):
    placed = (
        P(None, ("dp", "expert"), None),
        P(None, ("dp", "expert"), None),
        P(None, ("dp", "expert")),
        P(),
        P(None, ("dp", "expert")),
        P(),
        P(),
        P(),
        P(),
        P(),
        P(),
        P("expert", None, None),
        P("expert", None, None),
    )
    return jax.shard_map(
        per_device,
        mesh=mesh,
        in_specs=placed,
        out_specs=(
            P(None, ("dp", "expert"), None),
            P(None, ("dp", "expert"), None),
            P(),
            P(),
            P(),
            P(),
            P(),
            P(),
            P("expert", None, None),
            P("expert", None, None),
        ),
        check_vma=False,
    )
```

profile of v0, /device:TPU:0, one launch (start us, length us, event | category | flops | bytes accessed | tf_op | source)
XLA Modules:
  0.0 789.7 jit_solution(1991907835853382940)
XLA Ops:
  17.7 3.0 convolution_convert_fusion.10
  22.1 2.4 fusion
  31.8 2.5 gather_fusion
  36.2 3.9 scatter_custom_fusion
  40.1 5.7 all-to-all-start
  60.4 2.5 gather_fusion.2
  63.0 5.8 convolution_convert_fusion
  72.9 3.2 scatter_custom_fusion.1
  76.1 4.3 all-to-all-start.2
  80.5 3.3 scatter_custom_fusion.2
  83.8 3.1 scatter_custom_fusion.3
  88.1 9.2 %all-to-all-done.2 = bf16[8,96,768]{2,1,0:T(8,128)(2,1)S(1)} async-done(((bf16[8,96,768]{2,1,0:T(8,128)(2,1)}), bf16[8,96,768]{2,1,0:T(8,128)(2,1)S(1)}, u32[]{:S(2)}, u32[]{:S(2)}) %all-to-all-start.2) | async-done | bytes 1179680 | tf_op jit(solution)/shard_map/all_to_all | solution.py:111
  97.3 3.6 all-to-all-start.4
  100.9 12.6 %multiply_convert_fusion.3 = (bf16[768,3072]{1,0:T(8,128)(2,1)}, f32[768,3072]{1,0:T(8,128)}) fusion(bf16[768,768]{1,0:T(8,128)(2,1)} %bitcast.13, bf16[1,768,3072]{2,1,0:T(8,128)(2,1)} %param.28), kind=kOutput, calls=%fused_computation.16 | convolution fusion | flops 3635675136 | bytes 20054016 | tf_op jit(solution)/shard_map/dot_general | solution.py:114
  113.5 8.5 %fusion.12 = f32[768,3072]{1,0:T(8,128)} fusion(bf16[768,768]{1,0:T(8,128)(2,1)S(1)} %bitcast.311, bf16[1,768,3072]{2,1,0:T(8,128)(2,1)} %param.28), kind=kOutput, calls=%fused_computation.40 | convolution fusion | flops 3623878656 | bytes 15335424 | tf_op jit(solution)/shard_map/dot_general | solution.py:114
  122.0 4.1 all-to-all-start.6
  126.1 8.8 %multiply_convert_fusion.1 = bf16[768,3072]{1,0:T(8,128)(2,1)S(1)} fusion(f32[768,3072]{1,0:T(8,128)} %get-tuple-element.57, bf16[768,768]{1,0:T(8,128)(2,1)S(1)} %bitcast.314, bf16[1,3072,768]{2,1,0:T(8,128)(2,1)} %param.29), kind=kOutput, calls=%fused_computation.13 | convolution fusion | flops 3645112320 | bytes 20054016 | tf_op jit(solution)/shard_map/dot_general | solution.py:139
  135.0 10.2 %fusion.145 = f32[3072,768]{1,0:T(8,128)} fusion(bf16[768,3072]{1,0:T(8,128)(2,1)} %get-tuple-element.56, bf16[768,768]{1,0:T(8,128)(2,1)S(1)} %bitcast.315), kind=kOutput, calls=%fused_computation.230 | convolution fusion | flops 3623878656 | bytes 15335424 | tf_op jit(solution)/shard_map/dot_general | solution.py:136
  145.2 7.2 fusion.20
  152.4 4.4 all-to-all-start.5
  156.9 8.9 %multiply_convert_fusion = bf16[768,3072]{1,0:T(8,128)(2,1)S(1)} fusion(f32[768,3072]{1,0:T(8,128)} %fusion.12, bf16[768,768]{1,0:T(8,128)(2,1)S(1)} %bitcast.316, bf16[1,3072,768]{2,1,0:T(8,128)(2,1)} %param.29), kind=kOutput, calls=%fused_computation.12 | convolution fusion | flops 3645112320 | bytes 20054016 | tf_op jit(solution)/shard_map/dot_general | solution.py:139
  165.8 15.0 %fusion.17 = bf16[1,3072,768]{2,1,0:T(8,128)(2,1)} fusion(f32[3072,768]{1,0:T(8,128)} %fusion.145, bf16[768,768]{1,0:T(8,128)(2,1)S(1)} %bitcast.317, f32[768,3072]{1,0:T(8,128)} %fusion.12), kind=kOutput, calls=%fused_computation.45 | convolution fusion | flops 3640393728 | bytes 24772608 | tf_op jit(solution)/shard_map/dot_general | solution.py:136
  180.9 4.9 fusion.23
  185.7 4.6 all-to-all-start.7
  190.4 11.1 %fusion.29 = bf16[768,768]{1,0:T(8,128)(2,1)} fusion(bf16[1,3072,768]{2,1,0:T(8,128)(2,1)} %param.29, f32[768,3072]{1,0:T(8,128)} %fusion.12), kind=kOutput, calls=%fused_computation.59 | convolution fusion | flops 3636264960 | bytes 15335424 | tf_op jit(solution)/shard_map/dot_general | solution.py:116
  201.4 5.7 all-to-all-done.7
  207.2 4.3 all-to-all-start.3
  211.4 10.3 %fusion.144 = f32[768,3072]{1,0:T(8,128)} fusion(bf16[768,768]{1,0:T(8,128)(2,1)} %bitcast.13, bf16[768,3072]{1,0:T(8,128)(2,1)} %copy-done.26), kind=kOutput, calls=%fused_computation.229 | convolution fusion | flops 3623878656 | bytes 15335424 | tf_op jit(solution)/shard_map/dot_general | solution.py:141
  221.8 8.6 %fusion.26 = bf16[768,768]{1,0:T(8,128)(2,1)} fusion(bf16[768,3072]{1,0:T(8,128)(2,1)} %get-tuple-element.56, bf16[1,3072,768]{2,1,0:T(8,128)(2,1)} %param.29), kind=kOutput, calls=%fused_computation.58 | convolution fusion | flops 3624468480 | bytes 10616832 | tf_op jit(solution)/shard_map/dot_general | solution.py:116
  230.4 4.3 all-to-all-start.1
  234.9 11.5 %fusion.16 = bf16[1,768,3072]{2,1,0:T(8,128)(2,1)} fusion(f32[768,3072]{1,0:T(8,128)} %fusion.144, bf16[768,768]{1,0:T(8,128)(2,1)} %bitcast.312, bf16[768,3072]{1,0:T(8,128)(2,1)} %copy-done.92), kind=kOutput, calls=%fused_computation.44 | convolution fusion | flops 3628597248 | bytes 20054016 | tf_op jit(solution)/shard_map/dot_general | solution.py:141
  247.1 2.6 gather_fusion.5
  249.7 4.4 gather_fusion.3
  254.2 2.6 gather_fusion.4
  256.9 3.1 fusion.60
  260.6 4.4 gather_fusion.1
  265.0 4.2 fusion.70
  272.9 2.8 convolution_convert_fusion.5
  277.9 5.6 multiply_reduce_fusion.1
  298.3 2.4 multiply_convert_fusion.4
  321.8 2.6 fusion.57
  325.5 46.7 %all-reduce = (f32[768]{0:T(1024)}, f32[768]{0:T(1024)}) all-reduce(f32[768]{0:T(1024)} %add.207, f32[768]{0:T(1024)} %add.208), channel_id=1, replica_groups=mesh['dp'=4,'expert'=8] {'dp','expert'}, use_global_device_ids=true, to_apply=%region_30.33 | all-reduce | flops 1536 | bytes 12288 | tf_op jit(solution)/shard_map/psum | solution.py:208
  372.2 2.5 pad_maximum_fusion
  378.5 196.6 %all-reduce.8.cloned.1.call-done = (bf16[1,768,3072]{2,1,0:T(8,128)(2,1)}, bf16[1,3072,768]{2,1,0:T(8,128)(2,1)}) async-done(((bf16[1,768,3072]{2,1,0:T(8,128)(2,1)}, bf16[1,3072,768]{2,1,0:T(8,128)(2,1)}), (bf16[1,768,3072]{2,1,0:T(8,128)(2,1)}, bf16[1,3072,768]{2,1,0:T(8,128)(2,1)})) %all-reduce.8.cloned.1.call-update) | async-done | bytes 9437200 | tf_op jit(solution)/shard_map/psum | solution.py:220
  575.1 7.5 broadcast_in_dim.117
  582.6 4.9 broadcast_in_dim.119
  587.5 185.4 %all-reduce.6.cloned.1.call-done = (f32[768,768]{1,0:T(8,128)}, f32[768,768]{1,0:T(8,128)}, f32[768,768]{1,0:T(8,128)}, f32[768,768]{1,0:T(8,128)}) async-done(((f32[768,768]{1,0:T(8,128)}, f32[768,768]{1,0:T(8,128)}, f32[768,768]{1,0:T(8,128)}, f32[768,768]{1,0:T(8,128)}), (f32[768,768]{1,0:T(8,128)}, f32[768,768]{1,0:T(8,128)}, f32[768,768]{1,0:T(8,128)}, ...) | async-done | bytes 9437200 | tf_op jit(solution)/shard_map/psum | solution.py:208
  772.8 3.4 copy.69
  (293 shorter events, 94.8 us)
Async XLA Ops:
  8.9 36.9 %copy-start.79 = (f32[384]{0:T(512)}, f32[384]{0:T(512)S(1)}, u32[]{:S(2)}) copy-start(f32[384]{0:T(512)S(1)} %get-tuple-element.23) | copy-start | bytes 4612
  9.5 8.2 %copy-start.69 = (f32[384]{0:T(512)}, f32[384]{0:T(512)S(1)}, u32[]{:S(2)}) copy-start(f32[384]{0:T(512)S(1)} %fusion.115) | copy-start | bytes 4612
  11.0 3.8 copy-start.30
  17.7 4.4 copy-start.11
  24.5 2.9 copy-start.2
  26.0 3.4 copy-start.60
  31.1 5.1 copy-start.67
  31.7 8.4 %copy-start.73 = (f32[384]{0:T(512)}, f32[384]{0:T(512)S(1)}, u32[]{:S(2)}) copy-start(f32[384]{0:T(512)S(1)} %fusion.116) | copy-start | bytes 4612
  36.2 4.0 copy-start.89
  40.1 36.0 %all-to-all-start = ((bf16[8,96,768]{2,1,0:T(8,128)(2,1)}), bf16[8,96,768]{2,1,0:T(8,128)(2,1)}, u32[]{:S(2)}, u32[]{:S(2)}) async-start(bf16[8,96,768]{2,1,0:T(8,128)(2,1)} %bitcast.300), calls=%async_computation | async-start | bytes 2359296 | tf_op jit(solution)/shard_map/all_to_all | solution.py:111
  51.3 11.7 %copy-start.40 = (pred[384,384]{0,1:T(8,128)(4,1)}, pred[384,384]{0,1:T(8,128)(4,1)S(1)}, u32[]{:S(2)}) copy-start(pred[384,384]{0,1:T(8,128)(4,1)S(1)} %fusion.96) | copy-start | bytes 442372
  52.8 4.7 copy-start.15
  57.5 2.9 copy-start.3
  60.4 8.4 %copy-start.63 = (f32[12,384]{1,0:T(8,128)}, f32[12,384]{1,0:T(8,128)S(1)}, u32[]{:S(2)}) copy-start(f32[12,384]{1,0:T(8,128)S(1)} %log_add_fusion) | copy-start | bytes 55300
  72.2 3.9 copy-start.10
  72.2 3.9 copy-start.75
  76.1 4.4 copy-start.27
  76.1 4.4 copy-start.90
  76.1 21.2 %all-to-all-start.2 = ((bf16[8,96,768]{2,1,0:T(8,128)(2,1)}), bf16[8,96,768]{2,1,0:T(8,128)(2,1)S(1)}, u32[]{:S(2)}, u32[]{:S(2)}) async-start(bf16[8,96,768]{2,1,0:T(8,128)(2,1)} %bitcast.31), calls=%async_computation.2 | async-start | bytes 2359296 | tf_op jit(solution)/shard_map/all_to_all | solution.py:111
  97.3 16.2 %copy-start.54 = (bf16[8,96,768]{2,1,0:T(8,128)(2,1)}, bf16[8,96,768]{2,1,0:T(8,128)(2,1)S(1)}, u32[]{:S(2)}) copy-start(bf16[8,96,768]{2,1,0:T(8,128)(2,1)S(1)} %all-to-all-done.2) | copy-start | bytes 3538948
  97.3 24.7 %all-to-all-start.4 = ((bf16[8,96,768]{2,1,0:T(8,128)(2,1)}), bf16[8,96,768]{2,1,0:T(8,128)(2,1)S(1)}, u32[]{:S(2)}, u32[]{:S(2)}) async-start(bf16[8,96,768]{2,1,0:T(8,128)(2,1)} %bitcast.37), calls=%async_computation.4 | async-start | bytes 2359296 | tf_op jit(solution)/shard_map/all_to_all | solution.py:133
  122.0 30.4 %all-to-all-start.6 = ((bf16[8,96,768]{2,1,0:T(8,128)(2,1)}), bf16[8,96,768]{2,1,0:T(8,128)(2,1)S(1)}, u32[]{:S(2)}, u32[]{:S(2)}) async-start(bf16[8,96,768]{2,1,0:T(8,128)(2,1)} %bitcast.55), calls=%async_computation.6 | async-start | bytes 2359296 | tf_op jit(solution)/shard_map/all_to_all | solution.py:133
  134.9 10.3 %copy-start.26 = (bf16[768,3072]{1,0:T(8,128)(2,1)}, bf16[768,3072]{1,0:T(8,128)(2,1)S(1)}, u32[]{:S(2)}) copy-start(bf16[768,3072]{1,0:T(8,128)(2,1)S(1)} %multiply_convert_fusion.1) | copy-start | bytes 14155780
  152.4 33.3 %all-to-all-start.5 = ((bf16[8,96,768]{2,1,0:T(8,128)(2,1)}), bf16[8,96,768]{2,1,0:T(8,128)(2,1)S(1)}, u32[]{:S(2)}, u32[]{:S(2)}) async-start(bf16[8,96,768]{2,1,0:T(8,128)(2,1)} %bitcast.319), calls=%async_computation.5 | async-start | bytes 2359296 | tf_op jit(solution)/shard_map/all_to_all | solution.py:145
  156.8 24.0 %slice-start.4 = ((s8[4718592]{0:T(1024)(128)(4,1)}), s8[4194304]{0:T(1024)(128)(4,1)S(1)}, s32[]{:S(2)}) async-start(s8[4718592]{0:T(1024)(128)(4,1)} %bitcast.331), calls=%async_computation.14 | async-start | bytes 8388608
  165.8 15.0 %copy-start.92 = (bf16[768,3072]{1,0:T(8,128)(2,1)}, bf16[768,3072]{1,0:T(8,128)(2,1)S(1)}, u32[]{:S(2)}) copy-start(bf16[768,3072]{1,0:T(8,128)(2,1)S(1)} %multiply_convert_fusion) | copy-start | bytes 14155780
  165.8 15.0 %slice-start.5 = ((s8[4718592]{0:T(1024)(128)(4,1)}), s8[524288]{0:T(1024)(128)(4,1)S(1)}, s32[]{:S(2)}) async-start(s8[4718592]{0:T(1024)(128)(4,1)} %bitcast.331), calls=%async_computation.15 | async-start | bytes 1048576
  185.7 21.4 %all-to-all-start.7 = ((bf16[8,96,768]{2,1,0:T(8,128)(2,1)}), bf16[8,96,768]{2,1,0:T(8,128)(2,1)S(1)}, u32[]{:S(2)}, u32[]{:S(2)}) async-start(bf16[8,96,768]{2,1,0:T(8,128)(2,1)} %bitcast.320), calls=%async_computation.7 | async-start | bytes 2359296 | tf_op jit(solution)/shard_map/all_to_all | solution.py:145
  207.2 23.2 %all-to-all-start.3 = ((bf16[8,96,768]{2,1,0:T(8,128)(2,1)}), bf16[8,96,768]{2,1,0:T(8,128)(2,1)}, u32[]{:S(2)}, u32[]{:S(2)}) async-start(bf16[8,96,768]{2,1,0:T(8,128)(2,1)} %bitcast.318), calls=%async_computation.3 | async-start | bytes 2359296 | tf_op jit(solution)/shard_map/all_to_all | solution.py:117
  230.4 30.2 %all-to-all-start.1 = ((bf16[8,96,768]{2,1,0:T(8,128)(2,1)}), bf16[8,96,768]{2,1,0:T(8,128)(2,1)}, u32[]{:S(2)}, u32[]{:S(2)}) async-start(bf16[8,96,768]{2,1,0:T(8,128)(2,1)} %bitcast.313), calls=%async_computation.1 | async-start | bytes 2359296 | tf_op jit(solution)/shard_map/all_to_all | solution.py:117
  234.6 340.4 %all-reduce.8.cloned.1.call-start = ((), (), s32[]{:S(2)}) async-start(), calls=%async_computation.9 | async-start | bytes 18874368 | tf_op jit(solution)/shard_map/psum | solution.py:220
  246.4 526.4 %all-reduce.6.cloned.1.call-start = ((), (), s32[]{:S(2)}) async-start(), calls=%async_computation.8 | async-start | bytes 18874368 | tf_op jit(solution)/shard_map/psum | solution.py:208
  249.7 4.5 copy-start.81
  256.9 3.1 copy-start.86
  260.6 4.4 copy-start.88
  265.0 4.2 copy-start.29
  269.3 3.7 copy-start.6
  277.9 5.7 slice-start
  277.9 5.7 slice-start.1
  288.2 7.2 slice-start.2
  291.0 4.5 slice-start.3
  321.8 3.2 copy-start.83
  321.8 3.2 copy-start.84
  321.8 53.0 %copy-start.80 = (f32[384]{0:T(512)S(1)}, f32[384]{0:T(512)}, u32[]{:S(2)}) copy-start(f32[384]{0:T(512)} %copy-done.79) | copy-start | bytes 4612
  372.2 3.2 copy-start.8
  372.2 3.2 copy-start.36
  575.1 7.5 copy-start.25
  772.8 3.4 copy-start.46
  (61 other events, 108.2 us)
Sparse Core Ops, SparseCore 0:
  246.5 328.4 all-reduce.7
  581.9 190.9 all-reduce.5
where the time goes:
time: 799 us; the launch traced here: 790 us
  waiting for transfers between devices  397 us (50%)
  matrix products  184 us (23%)
  local copies, waits for them, and re-layouts  61.3 us (8%)
  other arithmetic  49.6 us (6%)
  blocking collectives  46.7 us (6%)
  starting transfers between devices  35.6 us (4%)
  between operations  15.4 us (2%)
    psum x1, waiting for transfers between devices, per_device(): lax.psum(grad_in_sum.astype(jnp.bfloat16), 'dp').astype(jnp.float32)  197 us
    psum x1, waiting for transfers between devices, per_device(): lax.psum((dense_total[0], dense_total[1], dense_total[2], dense_total[3],...  185 us
    psum x1, blocking collectives, per_device(): lax.psum((dense_total[0], dense_total[1], dense_total[2], dense_total[3],...  46.7 us
    dot_general x2, matrix products, per_device(): jnp.dot(active.T, grad_recv, preferred_element_type=float_type)  25.3 us
    dot_general x2, matrix products, per_device(): jnp.dot(received.T, grad_pre, preferred_element_type=float_type)  21.9 us
    dot_general x2, matrix products, per_device(): pre_active = jnp.dot(received, weight_in, preferred_element_type=float_type)  21.1 us
    unnamed x202, local copies, waits for them, and re-layouts  20.3 us
    dot_general x2, matrix products, per_device(): jnp.dot(active, weight_out, preferred_element_type=float_type)  19.7 us
  transfers between devices with their start and end apart: 10, of which 4 were waited for; matrix products, arithmetic and copies ran while one was open for 31% of the time, Pallas kernels for 0%

commit v1 on v0

--- a/solution.py
+++ b/solution.py
@@ -6,6 +6,12 @@
 HEADS = 12
 HEAD_DIM = 64
 epsilon = 1e-05
+
+
+def summed_here(shard, name):
+    shards = lax.all_gather(shard, name, axis=0, tiled=False)
+    summed = shards.sum(axis=0)
+    return summed
 
 
 def normalize(values, gain):
@@ -217,7 +223,7 @@
         ("dp", "expert"),
     )
     expert_in_sum, expert_out_sum = (
-        lax.psum(grad_in_sum.astype(jnp.bfloat16), "dp").astype(jnp.float32),
+        summed_here(grad_in_sum.astype(jnp.bfloat16), "dp").astype(jnp.float32),
         lax.psum(grad_out_sum.astype(jnp.bfloat16), "dp").astype(jnp.float32),
     )
     return (

time: 799 us -> 870 us (1.089)
  waiting for transfers between devices: 397 us -> 458 us
  other arithmetic: 49.6 us -> 62.2 us
  matrix products: 184 us -> 174 us
    all_gather x0 -> x1, waiting for transfers between devices: none -> 241 us  [summed_here(): shards = lax.all_gather(shard, name, axis=0, tiled=False)]
    psum x1, waiting for transfers between devices: 197 us -> 0.01 us  [per_device(): lax.psum(grad_out_sum.astype(jnp.bfloat16), 'dp').astype(jnp.float32)]
    all_to_all x2, waiting for transfers between devices: 0.01 us -> 15.1 us  [per_device(): lax.all_to_all(produced.reshape(owners, capacity, model_width), 'expert',...]
    reduce_sum x0 -> x1, other arithmetic: none -> 13.7 us  [summed_here(): summed = shards.sum(axis=0)]
    dot_general x2, matrix products: 21.9 us -> 12 us  [per_device(): jnp.dot(received.T, grad_pre, preferred_element_type=float_type)]
    psum x1, waiting for transfers between devices: 185 us -> 177 us  [per_device(): lax.psum((dense_total[0], dense_total[1], dense_total[2], dense_total[3],...]
    unnamed x202 -> x212, local copies, waits for them, and re-layouts: 20.3 us -> 23 us
  transfers between devices with their start and end apart: 10 -> 11, of which waited for: 4 -> 9; matrix products, arithmetic and copies ran while one was open for 31% -> 27% of each run, Pallas kernels for 0% -> 0%
where the time goes in v1:
time: 870 us; the launch traced here: 860 us
  waiting for transfers between devices  458 us (53%)
  matrix products  174 us (20%)
  local copies, waits for them, and re-layouts  65 us (7%)
  other arithmetic  62.2 us (7%)
  blocking collectives  51.3 us (6%)
  starting transfers between devices  34.4 us (4%)
  between operations  15.2 us (2%)
    all_gather x1, waiting for transfers between devices, summed_here(): shards = lax.all_gather(shard, name, axis=0, tiled=False)  241 us
    psum x1, waiting for transfers between devices, per_device(): lax.psum((dense_total[0], dense_total[1], dense_total[2], dense_total[3],...  177 us
    psum x1, blocking collectives, per_device(): lax.psum((dense_total[0], dense_total[1], dense_total[2], dense_total[3],...  51.3 us
    unnamed x212, local copies, waits for them, and re-layouts  23 us
    dot_general x2, matrix products, per_device(): pre_active = jnp.dot(received, weight_in, preferred_element_type=float_type)  21.3 us
    dot_general x2, matrix products, per_device(): jnp.dot(active.T, grad_recv, preferred_element_type=float_type)  21 us
    dot_general x2, matrix products, per_device(): jnp.dot(active, weight_out, preferred_element_type=float_type)  19.9 us
    dot_general x2, matrix products, per_device(): jnp.dot(grad_recv, weight_out.T, preferred_element_type=float_type)  17.7 us
  transfers between devices with their start and end apart: 11, of which 9 were waited for; matrix products, arithmetic and copies ran while one was open for 27% of the time, Pallas kernels for 0%

profile of v1, /device:TPU:0, one launch (start us, length us, event | category | flops | bytes accessed | tf_op | source)
XLA Modules:
  0.0 860.1 jit_solution(10636420905598548032)
XLA Ops:
  17.7 3.0 convolution_convert_fusion.10
  36.3 3.9 scatter_custom_fusion
  40.2 5.5 all-to-all-start
  50.0 3.7 scatter_custom_fusion.2
  63.0 3.7 scatter_custom_fusion.3
  71.8 4.9 all-to-all-start.4
  76.8 5.0 convolution_convert_fusion
  83.2 3.2 scatter_custom_fusion.1
  86.5 7.2 all-to-all-done.4
  93.6 3.6 all-to-all-start.2
  97.2 12.6 %multiply_convert_fusion.3 = (bf16[768,3072]{1,0:T(8,128)(2,1)}, f32[768,3072]{1,0:T(8,128)}) fusion(bf16[768,768]{1,0:T(8,128)(2,1)} %bitcast.13, bf16[1,768,3072]{2,1,0:T(8,128)(2,1)} %param.28), kind=kOutput, calls=%fused_computation.16 | convolution fusion | flops 3635675136 | bytes 20054016 | tf_op jit(solution)/shard_map/dot_general | solution.py:120
  109.8 4.2 all-to-all-done.2
  114.0 3.6 all-to-all-start.6
  117.8 8.7 %fusion.12 = f32[768,3072]{1,0:T(8,128)} fusion(bf16[768,768]{1,0:T(8,128)(2,1)S(1)} %bitcast.314, bf16[1,768,3072]{2,1,0:T(8,128)(2,1)} %param.28), kind=kOutput, calls=%fused_computation.41 | convolution fusion | flops 3623878656 | bytes 15335424 | tf_op jit(solution)/shard_map/dot_general | solution.py:120
  126.5 7.6 fusion.144
  134.3 13.4 %fusion.16 = bf16[1,3072,768]{2,1,0:T(8,128)(2,1)} fusion(f32[3072,768]{1,0:T(8,128)} %fusion.144, bf16[768,768]{1,0:T(8,128)(2,1)S(1)} %bitcast.316, f32[768,3072]{1,0:T(8,128)} %fusion.12), kind=kOutput, calls=%fused_computation.45 | convolution fusion | flops 3640393728 | bytes 24772608 | tf_op jit(solution)/shard_map/dot_general | solution.py:142
  147.9 8.9 %multiply_convert_fusion.1 = bf16[768,3072]{1,0:T(8,128)(2,1)S(1)} fusion(f32[768,3072]{1,0:T(8,128)} %get-tuple-element.55, bf16[768,768]{1,0:T(8,128)(2,1)} %bitcast.38, bf16[1,3072,768]{2,1,0:T(8,128)(2,1)} %param.29), kind=kOutput, calls=%fused_computation.13 | convolution fusion | flops 3645112320 | bytes 20054016 | tf_op jit(solution)/shard_map/dot_general | solution.py:145
  156.8 6.0 fusion.143
  162.9 8.9 %multiply_convert_fusion = bf16[768,3072]{1,0:T(8,128)(2,1)S(1)} fusion(f32[768,3072]{1,0:T(8,128)} %fusion.12, bf16[768,768]{1,0:T(8,128)(2,1)S(1)} %bitcast.317, bf16[1,3072,768]{2,1,0:T(8,128)(2,1)} %param.29), kind=kOutput, calls=%fused_computation.12 | convolution fusion | flops 3645112320 | bytes 20054016 | tf_op jit(solution)/shard_map/dot_general | solution.py:145
  173.9 6.0 add_convert_fusion.1
  179.9 8.6 %fusion.19 = bf16[768,768]{1,0:T(8,128)(2,1)} fusion(bf16[768,3072]{1,0:T(8,128)(2,1)} %copy-done.30, bf16[1,768,3072]{2,1,0:T(8,128)(2,1)} %param.28), kind=kOutput, calls=%fused_computation.56 | convolution fusion | flops 3624468480 | bytes 10616832 | tf_op jit(solution)/shard_map/dot_general | solution.py:148
  188.5 3.9 all-to-all-start.5
  192.4 8.8 %fusion.22 = bf16[768,768]{1,0:T(8,128)(2,1)} fusion(bf16[768,3072]{1,0:T(8,128)(2,1)} %copy-done.98, bf16[1,768,3072]{2,1,0:T(8,128)(2,1)} %param.28), kind=kOutput, calls=%fused_computation.57 | convolution fusion | flops 3624468480 | bytes 10616832 | tf_op jit(solution)/shard_map/dot_general | solution.py:148
  201.2 8.1 all-to-all-done.5
  209.3 3.6 all-to-all-start.7
  212.8 11.2 %fusion.28 = bf16[768,768]{1,0:T(8,128)(2,1)} fusion(bf16[1,3072,768]{2,1,0:T(8,128)(2,1)} %param.29, f32[768,3072]{1,0:T(8,128)} %fusion.12), kind=kOutput, calls=%fused_computation.59 | convolution fusion | flops 3636264960 | bytes 15335424 | tf_op jit(solution)/shard_map/dot_general | solution.py:122
  224.0 5.6 all-to-all-done.7
  229.6 4.4 all-to-all-start.3
  234.0 8.7 %fusion.25 = bf16[768,768]{1,0:T(8,128)(2,1)} fusion(bf16[768,3072]{1,0:T(8,128)(2,1)} %get-tuple-element.54, bf16[1,3072,768]{2,1,0:T(8,128)(2,1)} %param.29), kind=kOutput, calls=%fused_computation.58 | convolution fusion | flops 3624468480 | bytes 10616832 | tf_op jit(solution)/shard_map/dot_general | solution.py:122
  242.7 8.1 all-to-all-done.3
  250.8 4.4 all-to-all-start.1
  255.3 2.6 gather_fusion.5
  258.0 4.4 gather_fusion.3
  262.4 2.6 gather_fusion.4
  265.1 7.0 all-to-all-done.1
  272.1 4.6 gather_fusion.1
  276.8 2.8 fusion.59
  279.8 3.4 fusion.69
  286.8 2.8 convolution_convert_fusion.5
  291.8 5.7 multiply_reduce_fusion.1
  336.6 2.6 fusion.56
  340.4 51.3 %all-reduce = (f32[768]{0:T(1024)}, f32[768]{0:T(1024)}) all-reduce(f32[768]{0:T(1024)} %add.205, f32[768]{0:T(1024)} %add.206), channel_id=1, replica_groups=mesh['dp'=4,'expert'=8] {'dp','expert'}, use_global_device_ids=true, to_apply=%region_30.33 | all-reduce | flops 1536 | bytes 12288 | tf_op jit(solution)/shard_map/psum | solution.py:214
  397.9 6.9 broadcast_in_dim.112
  404.8 241.1 %all-gather.3.cloned.1.call-done = bf16[3072,3072]{1,0:T(8,128)(2,1)} async-done(((bf16[768,3072]{1,0:T(8,128)(2,1)}), bf16[3072,3072]{1,0:T(8,128)(2,1)}) %all-gather.3.cloned.1.call-update) | async-done | bytes 18874384 | tf_op jit(solution)/shard_map/all_gather | solution.py:12
  645.9 13.7 %reduce_sum.203 = bf16[768,3072]{1,0:T(8,128)(2,1)} reduce(bf16[4,768,3072]{2,1,0:T(8,128)(2,1)} %bitcast.286, bf16[]{:T(256)} %constant.58.clone.1), dimensions={0}, to_apply=%region_34.37 | reduce | flops 7077888 | bytes 23592962 | tf_op jit(solution)/shard_map/reduce_sum | solution.py:13
  659.6 7.4 bitcast_convert_fusion
  667.0 176.5 %all-reduce.7.cloned.1.call-done = (f32[768,768]{1,0:T(8,128)}, f32[768,768]{1,0:T(8,128)}, f32[768,768]{1,0:T(8,128)}, f32[768,768]{1,0:T(8,128)}) async-done(((f32[768,768]{1,0:T(8,128)}, f32[768,768]{1,0:T(8,128)}, f32[768,768]{1,0:T(8,128)}, f32[768,768]{1,0:T(8,128)}), (f32[768,768]{1,0:T(8,128)}, f32[768,768]{1,0:T(8,128)}, f32[768,768]{1,0:T(8,128)}, ...) | async-done | bytes 9437200 | tf_op jit(solution)/shard_map/psum | solution.py:214
  843.5 3.4 copy.68
  (306 shorter events, 107.3 us)
Async XLA Ops:
  8.9 36.8 %copy-start.83 = (f32[384]{0:T(512)}, f32[384]{0:T(512)S(1)}, u32[]{:S(2)}) copy-start(f32[384]{0:T(512)S(1)} %get-tuple-element.23) | copy-start | bytes 4612
  9.5 8.2 copy-start.73
  11.0 3.8 copy-start.34
  17.7 4.4 copy-start.14
  26.0 3.5 copy-start.64
  31.2 5.0 copy-start.71
  31.8 8.4 copy-start.77
  36.3 13.8 %copy-start.89 = (s32[384]{0:T(512)}, s32[384]{0:T(512)S(1)}, u32[]{:S(2)}) copy-start(s32[384]{0:T(512)S(1)} %get-tuple-element.35) | copy-start | bytes 4612
  40.2 31.6 %all-to-all-start = ((bf16[8,96,768]{2,1,0:T(8,128)(2,1)}), bf16[8,96,768]{2,1,0:T(8,128)(2,1)}, u32[]{:S(2)}, u32[]{:S(2)}) async-start(bf16[8,96,768]{2,1,0:T(8,128)(2,1)} %bitcast.303), calls=%async_computation | async-start | bytes 2359296 | tf_op jit(solution)/shard_map/all_to_all | solution.py:117
  54.9 21.9 %copy-start.44 = (pred[384,384]{0,1:T(8,128)(4,1)}, pred[384,384]{0,1:T(8,128)(4,1)S(1)}, u32[]{:S(2)}) copy-start(pred[384,384]{0,1:T(8,128)(4,1)S(1)} %fusion.95) | copy-start | bytes 442372
  56.3 10.3 %copy-start.18 = (bf16[384,768]{0,1:T(8,128)(2,1)}, bf16[384,768]{0,1:T(8,128)(2,1)S(1)}, u32[]{:S(2)}) copy-start(bf16[384,768]{0,1:T(8,128)(2,1)S(1)} %copy.43) | copy-start | bytes 1769476
  63.0 20.2 %copy-start.93 = (s32[384]{0:T(512)}, s32[384]{0:T(512)S(1)}, u32[]{:S(2)}) copy-start(s32[384]{0:T(512)S(1)} %get-tuple-element.37) | copy-start | bytes 4612
  71.8 5.0 copy-start.67
  71.8 5.0 copy-start.53
  71.8 21.8 %all-to-all-start.4 = ((bf16[8,96,768]{2,1,0:T(8,128)(2,1)}), bf16[8,96,768]{2,1,0:T(8,128)(2,1)}, u32[]{:S(2)}, u32[]{:S(2)}) async-start(bf16[8,96,768]{2,1,0:T(8,128)(2,1)} %bitcast.37), calls=%async_computation.4 | async-start | bytes 2359296 | tf_op jit(solution)/shard_map/all_to_all | solution.py:139
  76.8 5.0 copy-start.32
  82.6 3.8 copy-start.11
  83.2 3.2 copy-start.79
  93.6 20.3 %all-to-all-start.2 = ((bf16[8,96,768]{2,1,0:T(8,128)(2,1)}), bf16[8,96,768]{2,1,0:T(8,128)(2,1)S(1)}, u32[]{:S(2)}, u32[]{:S(2)}) async-start(bf16[8,96,768]{2,1,0:T(8,128)(2,1)} %bitcast.31), calls=%async_computation.2 | async-start | bytes 2359296 | tf_op jit(solution)/shard_map/all_to_all | solution.py:117
  114.0 20.3 %all-to-all-start.6 = ((bf16[8,96,768]{2,1,0:T(8,128)(2,1)}), bf16[8,96,768]{2,1,0:T(8,128)(2,1)S(1)}, u32[]{:S(2)}, u32[]{:S(2)}) async-start(bf16[8,96,768]{2,1,0:T(8,128)(2,1)} %bitcast.55), calls=%async_computation.6 | async-start | bytes 2359296 | tf_op jit(solution)/shard_map/all_to_all | solution.py:139
  117.5 280.4 %all-reduce.5.cloned.1.call-start = ((), (), s32[]{:S(2)}) async-start(), calls=%async_computation.8 | async-start | bytes 9437184 | tf_op jit(solution)/shard_map/psum | solution.py:227
  117.7 8.7 %copy-start.99 = (bf16[768,3072]{1,0:T(8,128)(2,1)S(1)}, bf16[768,3072]{1,0:T(8,128)(2,1)}, u32[]{:S(2)}) copy-start(bf16[768,3072]{1,0:T(8,128)(2,1)} %get-tuple-element.54) | copy-start | bytes 14155780
  147.7 498.2 %all-gather.3.cloned.1.call-start = ((), (), s32[]{:S(2)}) async-start(), calls=%async_computation.9 | async-start | bytes 23592960 | tf_op jit(solution)/shard_map/all_gather | solution.py:12
  156.8 6.0 copy-start.30
  188.5 20.7 %all-to-all-start.5 = ((bf16[8,96,768]{2,1,0:T(8,128)(2,1)}), bf16[8,96,768]{2,1,0:T(8,128)(2,1)S(1)}, u32[]{:S(2)}, u32[]{:S(2)}) async-start(bf16[8,96,768]{2,1,0:T(8,128)(2,1)} %bitcast.39), calls=%async_computation.5 | async-start | bytes 2359296 | tf_op jit(solution)/shard_map/all_to_all | solution.py:151
  209.3 20.3 %all-to-all-start.7 = ((bf16[8,96,768]{2,1,0:T(8,128)(2,1)}), bf16[8,96,768]{2,1,0:T(8,128)(2,1)S(1)}, u32[]{:S(2)}, u32[]{:S(2)}) async-start(bf16[8,96,768]{2,1,0:T(8,128)(2,1)} %bitcast.319), calls=%async_computation.7 | async-start | bytes 2359296 | tf_op jit(solution)/shard_map/all_to_all | solution.py:151
  229.6 21.3 %all-to-all-start.3 = ((bf16[8,96,768]{2,1,0:T(8,128)(2,1)}), bf16[8,96,768]{2,1,0:T(8,128)(2,1)}, u32[]{:S(2)}, u32[]{:S(2)}) async-start(bf16[8,96,768]{2,1,0:T(8,128)(2,1)} %bitcast.320), calls=%async_computation.3 | async-start | bytes 2359296 | tf_op jit(solution)/shard_map/all_to_all | solution.py:123
  250.8 4.5 copy-start.90
  250.8 4.5 copy-start.94
  250.8 21.2 %all-to-all-start.1 = ((bf16[8,96,768]{2,1,0:T(8,128)(2,1)}), bf16[8,96,768]{2,1,0:T(8,128)(2,1)}, u32[]{:S(2)}, u32[]{:S(2)}) async-start(bf16[8,96,768]{2,1,0:T(8,128)(2,1)} %bitcast.318), calls=%async_computation.1 | async-start | bytes 2359296 | tf_op jit(solution)/shard_map/all_to_all | solution.py:123
  255.2 588.3 %all-reduce.7.cloned.1.call-start = ((), (), s32[]{:S(2)}) async-start(), calls=%async_computation.10 | async-start | bytes 18874368 | tf_op jit(solution)/shard_map/psum | solution.py:214
  272.1 4.6 copy-start.9
  272.1 4.6 copy-start.12
  272.1 4.6 copy-start.72
  272.1 4.6 copy-start.78
  272.1 4.6 copy-start.80
  279.8 3.4 copy-start.33
  283.1 3.6 copy-start.6
  291.8 5.7 slice-start
  291.8 5.7 slice-start.1
  302.1 7.2 slice-start.2
  304.8 4.5 slice-start.3
  336.6 3.2 copy-start.85
  336.6 3.2 copy-start.86
  336.6 57.6 %copy-start.84 = (f32[384]{0:T(512)S(1)}, f32[384]{0:T(512)}, u32[]{:S(2)}) copy-start(f32[384]{0:T(512)} %copy-done.83) | copy-start | bytes 4612
  391.6 3.2 copy-start.8
  391.6 3.2 copy-start.40
  843.5 3.4 copy-start.50
  (67 other events, 127.8 us)
Sparse Core Ops, SparseCore 0:
  147.8 173.7 all-reduce.4
  323.2 322.6 all-gather.2
  652.7 190.7 all-reduce.6
